TPU v7x, 32 devices: a whole 2x2x4 slice. The times are simulated.
32 devices in a mesh: wide: 8 (over z, x), group: 4 (over y, core).
Axes of the slice: x: 2, y: 2, z: 4, core: 2. Of those that a mesh axis runs over, the one named last changes fastest.
Arguments:
- feat4: bfloat16 [32, 24, 24, 256], P(('wide', 'group')), may hold values from -100 to 100
- feat5: bfloat16 [32, 12, 12, 256], P(('wide', 'group')), may hold values from -100 to 100
- feat6: bfloat16 [32, 6, 6, 256], P(('wide', 'group')), may hold values from -100 to 100
- feat7: bfloat16 [32, 3, 3, 256], P(('wide', 'group')), may hold values from -100 to 100
- out_grad4: bfloat16 [32, 24, 24, 256], P(('wide', 'group')), may hold values from -6 to 6
- out_grad5: bfloat16 [32, 12, 12, 256], P(('wide', 'group')), may hold values from -6 to 6
- out_grad6: bfloat16 [32, 6, 6, 256], P(('wide', 'group')), may hold values from -6 to 6
- out_grad7: bfloat16 [32, 3, 3, 256], P(('wide', 'group')), may hold values from -6 to 6
- conv_weight: bfloat16 [3, 3, 256, 256], replicated, may hold values from -0.125 to 0.125
- bn_gain: float32 [4, 256], replicated, may hold values from 0.25 to 1.75
- bn_shift: float32 [4, 256], replicated, may hold values from -0.5 to 0.5
- heights: int32 [32], P(('wide', 'group')), may hold values from 168 to 384
- widths: int32 [32], P(('wide', 'group')), may hold values from 168 to 384
Outputs:
- out4: bfloat16 [32, 24, 24, 256], P(('wide', 'group'))
- out5: bfloat16 [32, 12, 12, 256], P(('wide', 'group'))
- out6: bfloat16 [32, 6, 6, 256], P(('wide', 'group'))
- out7: bfloat16 [32, 3, 3, 256], P(('wide', 'group'))
- d_feat4: bfloat16 [32, 24, 24, 256], P(('wide', 'group'))
- d_feat5: bfloat16 [32, 12, 12, 256], P(('wide', 'group'))
- d_feat6: bfloat16 [32, 6, 6, 256], P(('wide', 'group'))
- d_feat7: bfloat16 [32, 3, 3, 256], P(('wide', 'group'))
- d_weight: float32 [3, 3, 256, 256], replicated
- d_gain: float32 [4, 256], replicated
- d_shift: float32 [4, 256], replicated
Inputs may be any that keep to these rules, and one draw needn't show every extreme that they name: `heights`: pixel height of the valid part of each image. `widths`: pixel width of the valid part of each image.
All inputs are finite; a program needn't handle non-finite values.
Results may differ from a plain program's by a relative error of at most 0.0049.
Values sent between devices are 32-bit elements; how exact they have to be, the bound alone decides.
No kernel may reach another device: no remote copies, remote signals or barrier semaphores. Data moves between devices by JAX's collectives and lax.ppermute only.
A program may use at most 64 MiB of HBM per device.

v0:
```python
import jax
import jax.numpy as jnp
from jax import lax
from jax.sharding import PartitionSpec as P

EPSILON = 1e-05


def level_mask(heights, widths, stride, extent):
    row_limit = (heights[0] + stride - 1) // stride
    col_limit = (widths[0] + stride - 1) // stride
    row_place = lax.broadcasted_iota(jnp.int32, (extent, extent), 0)
    col_place = lax.broadcasted_iota(jnp.int32, (extent, extent), 1)
    inside = jnp.logical_and(row_place < row_limit, col_place < col_limit)
    return (inside.astype(jnp.float32), row_limit)


def conv_rows(padded, conv_weight, start_row, row_count, extent):
    summed = jnp.zeros((row_count * extent, conv_weight.shape[3]), jnp.float32)
    for tap_row in range(3):
        for tap_col in range(3):
            window = lax.dynamic_slice_in_dim(padded, start_row + tap_row, row_count, 0)[
                :, tap_col : tap_col + extent, :
            ]
            summed = summed + jnp.dot(
                window.reshape(row_count * extent, -1),
                conv_weight[tap_row, tap_col],
                preferred_element_type=jnp.float32,
            )
    return summed.reshape(row_count, extent, -1)


def input_grad_rows(padded_back, conv_weight, start_row, row_count, extent):
    summed = jnp.zeros((row_count * extent, conv_weight.shape[2]), jnp.float32)
    for tap_row in range(3):
        for tap_col in range(3):
            window = lax.dynamic_slice_in_dim(padded_back, start_row + 2 - tap_row, row_count, 0)[
                :, 2 - tap_col : 2 - tap_col + extent, :
            ]
            summed = summed + lax.dot_general(
                window.reshape(row_count * extent, -1),
                conv_weight[tap_row, tap_col],
                (((1,), (1,)), ((), ())),
                preferred_element_type=jnp.float32,
            )
    return summed.reshape(row_count, extent, -1)


def weight_grad_rows(padded, back_rows, start_row, row_count, extent):
    flat_back = back_rows.reshape(row_count * extent, -1)
    tap_terms = []
    for tap_row in range(3):
        for tap_col in range(3):
            window = lax.dynamic_slice_in_dim(padded, start_row + tap_row, row_count, 0)[
                :, tap_col : tap_col + extent, :
            ]
            tap_terms.append(
                lax.dot_general(
                    window.reshape(row_count * extent, -1),
                    flat_back,
                    (((0,), (0,)), ((), ())),
                    preferred_element_type=jnp.float32,
                )
            )
    return jnp.stack(tap_terms).reshape(3, 3, padded.shape[2], flat_back.shape[1])


def forward_conv(padded, conv_weight, extent):
    conv_out = conv_rows(padded, conv_weight, 0, extent, extent)
    return conv_out


def backward_conv(padded, back_grad, conv_weight, extent):
    padded_back = jnp.pad(back_grad, ((1, 1), (1, 1), (0, 0)))
    weight_part = weight_grad_rows(padded, back_grad, 0, extent, extent)
    input_part = input_grad_rows(padded_back, conv_weight, 0, extent, extent)
    return (weight_part, input_part)


def combine_stats(values):
    within = lax.psum(values, "group")
    result = lax.psum(within, "wide")
    return result


def combine_grads(values):
    within = lax.psum(values, "group")
    result = lax.psum(within, "wide")
    return result


def shards(
    feat4,
    feat5,
    feat6,
    feat7,
    out_grad4,
    out_grad5,
    out_grad6,
    out_grad7,
    conv_weight,
    bn_gain,
    bn_shift,
    heights,
    widths,
):
    features = (feat4, feat5, feat6, feat7)
    cotangents = (out_grad4, out_grad5, out_grad6, out_grad7)
    devices = lax.axis_size("wide") * lax.axis_size("group")
    levels = []
    for level_index in range(4):
        feature = features[level_index][0]
        extent = feature.shape[0]
        valid_mask, row_limit = level_mask(heights, widths, 16 * 2**level_index, extent)
        weighted = valid_mask[:, :, None]
        padded = jnp.pad(feature * weighted.astype(feature.dtype), ((1, 1), (1, 1), (0, 0)))
        conv_out = forward_conv(padded, conv_weight, extent)
        levels.append((valid_mask, row_limit, weighted, padded, conv_out))
    moments = []
    local_sums = jnp.stack(
        [jnp.sum(level_entry[4] * level_entry[2], axis=(0, 1)) for level_entry in levels]
    )
    local_squares = jnp.stack(
        [
            jnp.sum(level_entry[2] * level_entry[4] * level_entry[4], axis=(0, 1))
            for level_entry in levels
        ]
    )
    local_counts = jnp.stack([jnp.sum(level_entry[0]) for level_entry in levels])
    moment_sums, squares, counts = combine_stats((local_sums, local_squares, local_counts))
    for level_index in range(4):
        pixel_count = counts[level_index]
        mean_value = moment_sums[level_index] / pixel_count
        moments.append(
            (pixel_count, mean_value, squares[level_index] / pixel_count - mean_value * mean_value)
        )
    finals = []
    for level_index in range(4):
        valid_mask, row_limit, weighted, padded, conv_out = levels[level_index]
        pixel_count, mean_value, variance = moments[level_index]
        inverse = lax.rsqrt(variance + EPSILON)
        normed = (conv_out - mean_value) * inverse
        shifted = bn_gain[level_index] * normed + bn_shift[level_index]
        sigmoid_value = jax.nn.sigmoid(shifted)
        output = (weighted * shifted * sigmoid_value).astype(jnp.bfloat16)
        slope_term = (
            weighted
            * cotangents[level_index][0].astype(jnp.float32)
            * sigmoid_value
            * (1.0 + shifted * (1.0 - sigmoid_value))
        )
        finals.append((output, normed, inverse, slope_term))
    shift_local = jnp.stack([jnp.sum(final_entry[3], axis=(0, 1)) for final_entry in finals])
    gain_local = jnp.stack(
        [jnp.sum(final_entry[3] * final_entry[1], axis=(0, 1)) for final_entry in finals]
    )
    shift_rows, gain_rows = combine_stats((shift_local, gain_local))
    back_sums = [(shift_rows[level_index], gain_rows[level_index]) for level_index in range(4)]
    weight_local = jnp.zeros(conv_weight.shape, jnp.float32)
    outputs = []
    input_grads = []
    shift_list = []
    gain_list = []
    for level_index in range(4):
        valid_mask, row_limit, weighted, padded, conv_out = levels[level_index]
        pixel_count, mean_value, variance = moments[level_index]
        output, normed, inverse, slope_term = finals[level_index]
        shift_sum, gain_sum = back_sums[level_index]
        extent = conv_out.shape[0]
        back_grad = (
            weighted
            * (bn_gain[level_index] * inverse)
            * (slope_term - shift_sum / pixel_count - normed * (gain_sum / pixel_count))
        ).astype(jnp.bfloat16)
        weight_part, input_part = backward_conv(padded, back_grad, conv_weight, extent)
        weight_local = weight_local + weight_part
        input_grads.append((weighted * input_part).astype(jnp.bfloat16)[None])
        outputs.append(output[None])
        shift_list.append(shift_sum)
        gain_list.append(gain_sum)
    weight_total = combine_grads(weight_local)
    return (
        outputs[0],
        outputs[1],
        outputs[2],
        outputs[3],
        input_grads[0],
        input_grads[1],
        input_grads[2],
        input_grads[3],
        weight_total / devices,
        jnp.stack(gain_list) / devices,
        jnp.stack(shift_list) / devices,
    )


def solution(mesh):
    placed = (
        P(("wide", "group"), None, None, None),
        P(("wide", "group"), None, None, None),
        P(("wide", "group"), None, None, None),
        P(("wide", "group"), None, None, None),
        P(("wide", "group"), None, None, None),
        P(("wide", "group"), None, None, None),
        P(("wide", "group"), None, None, None),
        P(("wide", "group"), None, None, None),
        P(),
        P(),
        P(),
        P(("wide", "group")),
        P(("wide", "group")),
    )
    return jax.shard_map(
        shards,
        mesh=mesh,
        in_specs=placed,
        out_specs=(
            P(("wide", "group"), None, None, None),
            P(("wide", "group"), None, None, None),
            P(("wide", "group"), None, None, None),
            P(("wide", "group"), None, None, None),
            P(("wide", "group"), None, None, None),
            P(("wide", "group"), None, None, None),
            P(("wide", "group"), None, None, None),
            P(("wide", "group"), None, None, None),
            P(),
            P(),
            P(),
        ),
        check_vma=False,
    )
```

profile of v0, /device:TPU:0, one launch (start us, length us, event | category | flops | bytes accessed | tf_op | source)
XLA Modules:
  0.0 299.1 jit_solution(16657673691624110499)
XLA Ops:
  10.1 0.7 fusion.281
  11.5 0.8 bitcast_multiply_fusion.8
  12.2 0.8 broadcast_multiply_fusion.4
  13.8 0.7 fusion.257
  15.2 0.8 bitcast_multiply_fusion.6
  16.0 0.8 broadcast_multiply_fusion.3
  17.4 1.0 fusion.131
  18.4 1.1 convolution_add_fusion.63
  19.4 1.1 convolution_add_fusion.62
  21.9 0.7 multiply_reduce_fusion.6
  26.4 0.7 multiply_reduce_fusion.4
  31.1 0.7 reshape.1115
  35.5 2.6 pad_maximum_fusion.4
  38.2 8.7 %all-reduce.11 = (f32[4,256]{1,0:T(4,128)S(1)}, f32[4]{0:T(128)S(1)}, f32[4,256]{1,0:T(4,128)S(1)}) all-reduce(f32[4,256]{1,0:T(4,128)S(1)} %pad_maximum_fusion.1, f32[4]{0:T(128)S(1)} %pad_maximum_fusion.4, f32[4,256]{1,0:T(4,128)S(1)} %pad_maximum_fusion), channel_id=1, replica_groups=mesh['wide'=8,'group'=4] {'group'}, use_global_device_ids=true, to_apply=%region_16.17 | all-reduce | flops 2052 | bytes 16416 | tf_op jit(solution)/shard_map/psum | solution.py:81
  46.9 22.2 %all-reduce.9 = (f32[4,256]{1,0:T(4,128)S(1)}, f32[4]{0:T(128)S(1)}, f32[4,256]{1,0:T(4,128)S(1)}) all-reduce(f32[4,256]{1,0:T(4,128)S(1)} %get-tuple-element.34, f32[4]{0:T(128)S(1)} %get-tuple-element.35, f32[4,256]{1,0:T(4,128)S(1)} %get-tuple-element.36), channel_id=1, replica_groups=mesh['wide'=8,'group'=4] {'wide'}, use_global_device_ids=true, to_apply=%region_17.18 | all-reduce | flops 2052 | bytes 16416 | tf_op jit(solution)/shard_map/psum | solution.py:82
  69.7 2.6 slice_divide_fusion.8
  72.3 2.6 slice_divide_fusion.9
  78.2 0.7 fusion.299
  78.9 5.9 %all-reduce.10 = (f32[4,256]{1,0:T(4,128)S(1)}, f32[4,256]{1,0:T(4,128)S(1)}) all-reduce(f32[4,256]{1,0:T(4,128)S(1)} %pad_maximum_fusion.3, f32[4,256]{1,0:T(4,128)S(1)} %pad_maximum_fusion.2), channel_id=1, replica_groups=mesh['wide'=8,'group'=4] {'group'}, use_global_device_ids=true, to_apply=%region_28.29 | all-reduce | flops 2048 | bytes 16384 | tf_op jit(solution)/shard_map/psum | solution.py:81
  84.8 17.6 %all-reduce.8 = (f32[4,256]{1,0:T(4,128)S(1)}, f32[4,256]{1,0:T(4,128)S(1)}) all-reduce(f32[4,256]{1,0:T(4,128)S(1)} %get-tuple-element.32, f32[4,256]{1,0:T(4,128)S(1)} %get-tuple-element.33), channel_id=1, replica_groups=mesh['wide'=8,'group'=4] {'wide'}, use_global_device_ids=true, to_apply=%region_29.30 | all-reduce | flops 2048 | bytes 16384 | tf_op jit(solution)/shard_map/psum | solution.py:82
  102.4 2.6 slice_divide_fusion
  105.1 2.6 slice_divide_fusion.1
  107.9 1.1 multiply_convert_fusion.2
  120.9 2.1 add_add_fusion
  127.0 1.3 reshape.1156
  128.3 1.3 reshape.1150
  129.6 1.3 reshape.1151
  130.9 1.3 reshape.1152
  132.2 1.3 reshape.1153
  133.5 0.7 reshape.1154
  135.0 0.9 convolution_add_fusion.55
  135.9 0.9 convolution_add_fusion.54
  136.8 0.9 convolution_add_fusion.53
  137.6 1.0 convolution_add_fusion.52
  138.6 0.9 convolution_add_fusion.51
  140.1 1.4 multiply_convert_fusion.21
  145.3 0.9 convolution_add_fusion.39
  146.2 0.9 convolution_add_fusion.38
  147.1 0.9 convolution_add_fusion.37
  148.1 1.0 convolution_add_fusion.36
  152.4 0.7 reshape.1139
  153.2 1.2 pad_slice_fusion
  154.4 0.7 multiply_convert_fusion.13
  156.1 20.6 %all-reduce.15.cloned.1.call-done = f32[3,3,256,256]{3,2,1,0:T(8,128)} async-done(((f32[3,3,256,256]{3,2,1,0:T(8,128)}), f32[3,3,256,256]{3,2,1,0:T(8,128)}) %all-reduce.15.cloned.1.call-update) | async-done | bytes 2359312 | tf_op jit(solution)/shard_map/psum | solution.py:87
  176.7 1.9 multiply_convert_fusion.6
  181.7 1.1 multiply_convert_fusion.1
  182.7 106.2 %all-reduce.17.cloned.1.call-done = f32[3,3,256,256]{3,2,1,0:T(8,128)} async-done(((f32[3,3,256,256]{3,2,1,0:T(8,128)}), f32[3,3,256,256]{3,2,1,0:T(8,128)}) %all-reduce.17.cloned.1.call-update) | async-done | bytes 2359312 | tf_op jit(solution)/shard_map/psum | solution.py:88
  289.0 3.3 %broadcast_multiply_fusion = f32[3,3,256,256]{3,2,1,0:T(8,128)} fusion(f32[3,3,256,256]{3,2,1,0:T(8,128)} %all-reduce.17.cloned.1.call-done), kind=kLoop, calls=%fused_computation.17 | loop fusion | flops 589824 | bytes 4718592 | tf_op jit(solution)/shard_map/div | solution.py:191
  (476 shorter events, 47.3 us)
Async XLA Ops:
  7.2 13.3 %copy-start = (bf16[3,3,256,256]{3,2,1,0:T(8,128)(2,1)S(1)}, bf16[3,3,256,256]{3,2,1,0:T(8,128)(2,1)}, u32[]{:S(2)}) copy-start(bf16[3,3,256,256]{3,2,1,0:T(8,128)(2,1)} %param.21) | copy-start | bytes 3538948
  7.2 16.6 %copy-start.9 = (bf16[1,12,12,256]{3,2,1,0:T(8,128)(2,1)S(1)}, bf16[1,12,12,256]{3,2,1,0:T(8,128)(2,1)}, u32[]{:S(2)}) copy-start(bf16[1,12,12,256]{3,2,1,0:T(8,128)(2,1)} %param.14) | copy-start | bytes 221188
  7.2 169.5 %all-reduce.15.cloned.1.call-start = ((), (), s32[]{:S(2)}) async-start(), calls=%async_computation | async-start | bytes 4718592 | tf_op jit(solution)/shard_map/psum | solution.py:87
  16.0 8.5 %copy-start.28 = (bf16[6,6,256]{2,1,0:T(8,128)(2,1)}, bf16[6,6,256]{2,1,0:T(8,128)(2,1)S(1)}, u32[]{:S(2)}) copy-start(bf16[6,6,256]{2,1,0:T(8,128)(2,1)S(1)} %bitcast_multiply_fusion.6) | copy-start | bytes 55300
  16.8 7.6 %copy-start.33 = (bf16[1,6,6,256]{3,2,1,0:T(8,128)(2,1)}, bf16[1,6,6,256]{3,2,1,0:T(8,128)(2,1)S(1)}, u32[]{:S(2)}) copy-start(bf16[1,6,6,256]{3,2,1,0:T(8,128)(2,1)S(1)} %broadcast_multiply_fusion.3) | copy-start | bytes 55300
  24.0 4.5 %copy-start.12 = (bf16[1,12,12,256]{3,2,1,0:T(8,128)(2,1)}, bf16[1,12,12,256]{3,2,1,0:T(8,128)(2,1)S(1)}, u32[]{:S(2)}) copy-start(bf16[1,12,12,256]{3,2,1,0:T(8,128)(2,1)S(1)} %broadcast_multiply_fusion.2) | copy-start | bytes 221188
  32.2 45.2 %copy-start.45 = (f32[1,256]{1,0:T(1,128)}, f32[1,256]{1,0:T(1,128)S(1)}, u32[]{:S(2)}) copy-start(f32[1,256]{1,0:T(1,128)S(1)} %get-tuple-element.118) | copy-start | bytes 3076
  32.2 45.6 %copy-start.66 = (f32[1,256]{1,0:T(1,128)}, f32[1,256]{1,0:T(1,128)S(1)}, u32[]{:S(2)}) copy-start(f32[1,256]{1,0:T(1,128)S(1)} %get-tuple-element.117) | copy-start | bytes 3076
  32.2 45.7 %copy-start.69 = (f32[1,256]{1,0:T(1,128)}, f32[1,256]{1,0:T(1,128)S(1)}, u32[]{:S(2)}) copy-start(f32[1,256]{1,0:T(1,128)S(1)} %get-tuple-element.119) | copy-start | bytes 3076
  32.2 45.9 %copy-start.98 = (f32[1,256]{1,0:T(1,128)}, f32[1,256]{1,0:T(1,128)S(1)}, u32[]{:S(2)}) copy-start(f32[1,256]{1,0:T(1,128)S(1)} %get-tuple-element.116) | copy-start | bytes 3076
  32.3 45.1 %copy-start.56 = (f32[1,256]{1,0:T(1,128)}, f32[1,256]{1,0:T(1,128)S(1)}, u32[]{:S(2)}) copy-start(f32[1,256]{1,0:T(1,128)S(1)} %get-tuple-element.130) | copy-start | bytes 3076
  32.3 45.5 %copy-start.84 = (f32[1,256]{1,0:T(1,128)}, f32[1,256]{1,0:T(1,128)S(1)}, u32[]{:S(2)}) copy-start(f32[1,256]{1,0:T(1,128)S(1)} %get-tuple-element.129) | copy-start | bytes 3076
  32.3 45.7 %copy-start.87 = (f32[1,256]{1,0:T(1,128)}, f32[1,256]{1,0:T(1,128)S(1)}, u32[]{:S(2)}) copy-start(f32[1,256]{1,0:T(1,128)S(1)} %get-tuple-element.131) | copy-start | bytes 3076
  32.3 45.8 %copy-start.100 = (f32[1,256]{1,0:T(1,128)}, f32[1,256]{1,0:T(1,128)S(1)}, u32[]{:S(2)}) copy-start(f32[1,256]{1,0:T(1,128)S(1)} %get-tuple-element.128) | copy-start | bytes 3076
  34.6 42.8 %copy-start.1 = (bf16[1,24,24,256]{3,2,1,0:T(8,128)(2,1)S(1)}, bf16[1,24,24,256]{3,2,1,0:T(8,128)(2,1)}, u32[]{:S(2)}) copy-start(bf16[1,24,24,256]{3,2,1,0:T(8,128)(2,1)} %param.17) | copy-start | bytes 884740
  34.6 42.8 %copy-start.18 = (f32[24,24]{1,0:T(8,128)S(1)}, f32[24,24]{1,0:T(8,128)}, u32[]{:S(2)}) copy-start(f32[24,24]{1,0:T(8,128)} %get-tuple-element.150) | copy-start | bytes 6916
  35.2 42.6 %copy-start.7 = (bf16[1,12,12,256]{3,2,1,0:T(8,128)(2,1)S(1)}, bf16[1,12,12,256]{3,2,1,0:T(8,128)(2,1)}, u32[]{:S(2)}) copy-start(bf16[1,12,12,256]{3,2,1,0:T(8,128)(2,1)} %param.18) | copy-start | bytes 221188
  35.2 42.8 %copy-start.16 = (bf16[1,6,6,256]{3,2,1,0:T(8,128)(2,1)S(1)}, bf16[1,6,6,256]{3,2,1,0:T(8,128)(2,1)}, u32[]{:S(2)}) copy-start(bf16[1,6,6,256]{3,2,1,0:T(8,128)(2,1)} %param.19) | copy-start | bytes 55300
  35.2 42.8 %copy-start.37 = (f32[6,6]{1,0:T(8,128)S(1)}, f32[6,6]{1,0:T(8,128)}, u32[]{:S(2)}) copy-start(f32[6,6]{1,0:T(8,128)} %get-tuple-element.146) | copy-start | bytes 436
  35.2 43.0 %copy-start.26 = (f32[3,3,256]{2,1,0:T(4,128)S(1)}, f32[3,3,256]{2,1,0:T(4,128)}, u32[]{:S(2)}) copy-start(f32[3,3,256]{2,1,0:T(4,128)} %reshape.1121) | copy-start | bytes 27652
  35.2 43.0 %copy-start.48 = (f32[3,3]{1,0:T(4,128)S(1)}, f32[3,3]{1,0:T(4,128)}, u32[]{:S(2)}) copy-start(f32[3,3]{1,0:T(4,128)} %get-tuple-element.144) | copy-start | bytes 112
  35.2 43.0 %copy-start.74 = (bf16[1,3,3,256]{3,2,1,0:T(4,128)(2,1)S(1)}, bf16[1,3,3,256]{3,2,1,0:T(4,128)(2,1)}, u32[]{:S(2)}) copy-start(bf16[1,3,3,256]{3,2,1,0:T(4,128)(2,1)} %param.20) | copy-start | bytes 13828
  75.0 32.8 %copy-start.42 = (f32[1,256]{1,0:T(1,128)}, f32[1,256]{1,0:T(1,128)S(1)}, u32[]{:S(2)}) copy-start(f32[1,256]{1,0:T(1,128)S(1)} %get-tuple-element.123) | copy-start | bytes 3076
  75.0 32.8 %copy-start.60 = (f32[1,256]{1,0:T(1,128)}, f32[1,256]{1,0:T(1,128)S(1)}, u32[]{:S(2)}) copy-start(f32[1,256]{1,0:T(1,128)S(1)} %get-tuple-element.122) | copy-start | bytes 3076
  75.0 32.8 %copy-start.63 = (f32[1,256]{1,0:T(1,128)}, f32[1,256]{1,0:T(1,128)S(1)}, u32[]{:S(2)}) copy-start(f32[1,256]{1,0:T(1,128)S(1)} %get-tuple-element.121) | copy-start | bytes 3076
  75.0 32.8 %copy-start.72 = (f32[1,256]{1,0:T(1,128)}, f32[1,256]{1,0:T(1,128)S(1)}, u32[]{:S(2)}) copy-start(f32[1,256]{1,0:T(1,128)S(1)} %get-tuple-element.120) | copy-start | bytes 3076
  75.6 32.2 %copy-start.81 = (f32[256]{0:T(256)}, f32[256]{0:T(256)S(1)}, u32[]{:S(2)}) copy-start(f32[256]{0:T(256)S(1)} %get-tuple-element.137) | copy-start | bytes 3076
  76.2 31.6 %copy-start.92 = (f32[256]{0:T(256)}, f32[256]{0:T(256)S(1)}, u32[]{:S(2)}) copy-start(f32[256]{0:T(256)S(1)} %get-tuple-element.135) | copy-start | bytes 3076
  76.8 31.1 %copy-start.78 = (f32[256]{0:T(256)}, f32[256]{0:T(256)S(1)}, u32[]{:S(2)}) copy-start(f32[256]{0:T(256)S(1)} %get-tuple-element.139) | copy-start | bytes 3076
  77.4 30.5 %copy-start.52 = (f32[256]{0:T(256)}, f32[256]{0:T(256)S(1)}, u32[]{:S(2)}) copy-start(f32[256]{0:T(256)S(1)} %get-tuple-element.141) | copy-start | bytes 3076
  102.4 5.5 %copy-start.94 = (f32[4,256]{1,0:T(4,128)}, f32[4,256]{1,0:T(4,128)S(1)}, u32[]{:S(2)}) copy-start(f32[4,256]{1,0:T(4,128)S(1)} %get-tuple-element.28) | copy-start | bytes 12292
  102.4 5.5 %copy-start.96 = (f32[4,256]{1,0:T(4,128)}, f32[4,256]{1,0:T(4,128)S(1)}, u32[]{:S(2)}) copy-start(f32[4,256]{1,0:T(4,128)S(1)} %get-tuple-element.27) | copy-start | bytes 12292
  105.0 5.3 %copy-start.104 = (f32[1,256]{1,0:T(1,128)}, f32[1,256]{1,0:T(1,128)S(1)}, u32[]{:S(2)}) copy-start(f32[1,256]{1,0:T(1,128)S(1)} %get-tuple-element.113) | copy-start | bytes 3076
  105.0 9.1 %copy-start.115 = (f32[1,256]{1,0:T(1,128)}, f32[1,256]{1,0:T(1,128)S(1)}, u32[]{:S(2)}) copy-start(f32[1,256]{1,0:T(1,128)S(1)} %get-tuple-element.111) | copy-start | bytes 3076
  105.1 11.6 %copy-start.122 = (f32[1,256]{1,0:T(1,128)}, f32[1,256]{1,0:T(1,128)S(1)}, u32[]{:S(2)}) copy-start(f32[1,256]{1,0:T(1,128)S(1)} %get-tuple-element.110) | copy-start | bytes 3076
  105.1 14.1 %copy-start.111 = (f32[1,256]{1,0:T(1,128)}, f32[1,256]{1,0:T(1,128)S(1)}, u32[]{:S(2)}) copy-start(f32[1,256]{1,0:T(1,128)S(1)} %get-tuple-element.112) | copy-start | bytes 3076
  107.7 6.4 %copy-start.116 = (f32[1,256]{1,0:T(1,128)}, f32[1,256]{1,0:T(1,128)S(1)}, u32[]{:S(2)}) copy-start(f32[1,256]{1,0:T(1,128)S(1)} %get-tuple-element.107) | copy-start | bytes 3076
  107.7 9.0 %copy-start.123 = (f32[1,256]{1,0:T(1,128)}, f32[1,256]{1,0:T(1,128)S(1)}, u32[]{:S(2)}) copy-start(f32[1,256]{1,0:T(1,128)S(1)} %get-tuple-element.106) | copy-start | bytes 3076
  107.7 11.4 %copy-start.113 = (f32[1,256]{1,0:T(1,128)}, f32[1,256]{1,0:T(1,128)S(1)}, u32[]{:S(2)}) copy-start(f32[1,256]{1,0:T(1,128)S(1)} %get-tuple-element.108) | copy-start | bytes 3076
  123.0 14.6 %copy-start.25 = (f32[9,256]{1,0:T(8,128)S(1)}, f32[9,256]{1,0:T(8,128)}, u32[]{:S(2)}) copy-start(f32[9,256]{1,0:T(8,128)} %copy-done.24) | copy-start | bytes 27652
  123.0 165.9 %all-reduce.17.cloned.1.call-start = ((), (), s32[]{:S(2)}) async-start(), calls=%async_computation.1 | async-start | bytes 4718592 | tf_op jit(solution)/shard_map/psum | solution.py:88
  126.9 14.5 %copy-start.32 = (bf16[6,6,256]{2,1,0:T(8,128)(2,1)S(1)}, bf16[6,6,256]{2,1,0:T(8,128)(2,1)}, u32[]{:S(2)}) copy-start(bf16[6,6,256]{2,1,0:T(8,128)(2,1)} %get-tuple-element.70) | copy-start | bytes 55300
  126.9 14.5 %copy-start.31 = (bf16[6,6,256]{2,1,0:T(8,128)(2,1)S(1)}, bf16[6,6,256]{2,1,0:T(8,128)(2,1)}, u32[]{:S(2)}) copy-start(bf16[6,6,256]{2,1,0:T(8,128)(2,1)} %get-tuple-element.71) | copy-start | bytes 55300
  127.0 15.2 %copy-start.30 = (bf16[6,6,256]{2,1,0:T(8,128)(2,1)S(1)}, bf16[6,6,256]{2,1,0:T(8,128)(2,1)}, u32[]{:S(2)}) copy-start(bf16[6,6,256]{2,1,0:T(8,128)(2,1)} %get-tuple-element.72) | copy-start | bytes 55300
  134.8 4.8 %copy-start.51 = (bf16[9,256]{1,0:T(8,128)(2,1)S(1)}, bf16[9,256]{1,0:T(8,128)(2,1)}, u32[]{:S(2)}) copy-start(bf16[9,256]{1,0:T(8,128)(2,1)} %reshape.1155) | copy-start | bytes 13828
  134.8 5.0 %copy-start.50 = (bf16[9,256]{1,0:T(8,128)(2,1)S(1)}, bf16[9,256]{1,0:T(8,128)(2,1)}, u32[]{:S(2)}) copy-start(bf16[9,256]{1,0:T(8,128)(2,1)} %reshape.1156) | copy-start | bytes 13828
  144.9 4.2 %copy-start.36 = (bf16[36,256]{1,0:T(8,128)(2,1)S(1)}, bf16[36,256]{1,0:T(8,128)(2,1)}, u32[]{:S(2)}) copy-start(bf16[36,256]{1,0:T(8,128)(2,1)} %reshape.1144) | copy-start | bytes 55300
  145.0 4.4 %copy-start.35 = (bf16[36,256]{1,0:T(8,128)(2,1)S(1)}, bf16[36,256]{1,0:T(8,128)(2,1)}, u32[]{:S(2)}) copy-start(bf16[36,256]{1,0:T(8,128)(2,1)} %reshape.1145) | copy-start | bytes 55300
  (81 other events, 139.4 us)
Sparse Core Ops, SparseCore 0:
  123.2 53.5 all-reduce.14
  180.3 108.6 all-reduce.16
where the time goes:
time: 301 us; the launch traced here: 299 us
  waiting for transfers between devices  127 us (42%)
  blocking collectives  54.4 us (18%)
  other arithmetic  41.2 us (14%)
  matrix products  34 us (11%)
  local copies, waits for them, and re-layouts  24.6 us (8%)
  between operations  18.1 us (6%)
    psum x1, waiting for transfers between devices, combine_grads(): result = lax.psum(within, 'wide')  106 us
    psum x2, blocking collectives, combine_stats(): result = lax.psum(within, 'wide')  39.7 us
    psum x1, waiting for transfers between devices, combine_grads(): within = lax.psum(values, 'group')  20.6 us
    psum x2, blocking collectives, combine_stats(): within = lax.psum(values, 'group')  14.6 us
    dot_general x36, matrix products, input_grad_rows(): lax.dot_general(window.reshape(row_count * extent, -1), conv_weight[tap_r...  14.1 us
    reshape x24, local copies, waits for them, and re-layouts, input_grad_rows(): window.reshape(row_count * extent, -1)  11.1 us
    dot_general x36, matrix products, conv_rows(): jnp.dot(window.reshape(row_count * extent, -1), conv_weight[tap_row, tap_...  10.4 us
    dot_general x36, matrix products, weight_grad_rows(): lax.dot_general(window.reshape(row_count * extent, -1), flat_back, (((0,)...  9.51 us
  transfers between devices with their start and end apart: 2, of which 2 were waited for; matrix products, arithmetic and copies ran while one was open for 12% of the time, Pallas kernels for 0%

commit v1 on v0

--- a/solution.py
+++ b/solution.py
@@ -4,6 +4,14 @@
 from jax.sharding import PartitionSpec as P
 
 EPSILON = 1e-05
+
+
+def sum_by_hops(array, name):
+    count, acc = (lax.axis_size(name), array)
+    for reach in [1 << k for k in range(count.bit_length() - 1)]:
+        swap = [(i, i ^ reach) for i in range(count)]
+        acc = acc + lax.ppermute(acc, name, swap)
+    return acc
 
 
 def level_mask(heights, widths, stride, extent):
@@ -85,7 +93,7 @@
 
 def combine_grads(values):
     within = lax.psum(values, "group")
-    result = lax.psum(within, "wide")
+    result = sum_by_hops(within, "wide")
     return result
 
 

time: 301 us -> 399 us (1.33)
  waiting for transfers between devices: 127 us -> 234 us
  local copies, waits for them, and re-layouts: 24.6 us -> 14.1 us
  starting transfers between devices: 0.08 us -> 5.46 us
  matrix products: 34 us -> 29.3 us
    ppermute x0 -> x3, waiting for transfers between devices: none -> 184 us  [sum_by_hops(): acc = acc + lax.ppermute(acc, name, swap)]
    psum x1 -> x0, waiting for transfers between devices: 106 us -> none  [combine_grads(): result = lax.psum(within, 'wide')]
    psum x1, waiting for transfers between devices: 20.6 us -> 49.5 us  [combine_grads(): within = lax.psum(values, 'group')]
    reshape x24, local copies, waits for them, and re-layouts: 11.1 us -> 3.2 us  [input_grad_rows(): window.reshape(row_count * extent, -1)]
    add x0 -> x2, other arithmetic: none -> 6.06 us  [sum_by_hops(): acc = acc + lax.ppermute(acc, name, swap)]
    ppermute x0 -> x3, starting transfers between devices: none -> 5.42 us  [sum_by_hops(): acc = acc + lax.ppermute(acc, name, swap)]
    dot_general x36, matrix products: 14.1 us -> 9.39 us  [input_grad_rows(): lax.dot_general(window.reshape(row_count * extent, -1), conv_weight[tap_r...]
  transfers between devices with their start and end apart: 2 -> 4, of which waited for: 2 -> 4; matrix products, arithmetic and copies ran while one was open for 12% -> 5% of each run, Pallas kernels for 0% -> 0%
where the time goes in v1:
time: 399 us; the launch traced here: 398 us
  waiting for transfers between devices  234 us (59%)
  blocking collectives  54.3 us (14%)
  other arithmetic  42.7 us (11%)
  matrix products  29.3 us (7%)
  between operations  18.2 us (5%)
  local copies, waits for them, and re-layouts  14.1 us (4%)
  starting transfers between devices  5.46 us (1%)
    ppermute x3, waiting for transfers between devices, sum_by_hops(): acc = acc + lax.ppermute(acc, name, swap)  184 us
    psum x1, waiting for transfers between devices, combine_grads(): within = lax.psum(values, 'group')  49.5 us
    psum x2, blocking collectives, combine_stats(): result = lax.psum(within, 'wide')  39.7 us
    psum x2, blocking collectives, combine_stats(): within = lax.psum(values, 'group')  14.6 us
    dot_general x36, matrix products, conv_rows(): jnp.dot(window.reshape(row_count * extent, -1), conv_weight[tap_row, tap_...  10.4 us
    dot_general x36, matrix products, weight_grad_rows(): lax.dot_general(window.reshape(row_count * extent, -1), flat_back, (((0,)...  9.51 us
    dot_general x36, matrix products, input_grad_rows(): lax.dot_general(window.reshape(row_count * extent, -1), conv_weight[tap_r...  9.39 us
  transfers between devices with their start and end apart: 4, of which 4 were waited for; matrix products, arithmetic and copies ran while one was open for 5% of the time, Pallas kernels for 0%

profile of v1, /device:TPU:0, one launch (start us, length us, event | category | flops | bytes accessed | tf_op | source)
XLA Modules:
  0.0 398.0 jit_solution(6705998173099270674)
XLA Ops:
  8.7 0.7 fusion.283
  10.1 0.7 fusion.281
  10.8 0.7 and_convert_fusion.3
  11.5 0.8 bitcast_multiply_fusion.8
  12.2 0.8 broadcast_multiply_fusion.3
  13.0 0.7 fusion.268
  13.8 0.7 fusion.257
  14.5 0.7 and_convert_fusion
  15.2 0.8 bitcast_multiply_fusion.6
  16.0 0.8 broadcast_multiply_fusion.2
  17.4 1.0 fusion.131
  18.4 1.1 convolution_add_fusion.63
  19.5 1.1 convolution_add_fusion.62
  21.9 0.7 multiply_reduce_fusion.6
  26.5 0.7 multiply_reduce_fusion.4
  31.1 0.7 reshape.1115
  35.5 2.6 pad_maximum_fusion.4
  38.2 8.7 %all-reduce.11 = (f32[4,256]{1,0:T(4,128)S(1)}, f32[4]{0:T(128)S(1)}, f32[4,256]{1,0:T(4,128)S(1)}) all-reduce(f32[4,256]{1,0:T(4,128)S(1)} %pad_maximum_fusion.1, f32[4]{0:T(128)S(1)} %pad_maximum_fusion.4, f32[4,256]{1,0:T(4,128)S(1)} %pad_maximum_fusion), channel_id=1, replica_groups=mesh['wide'=8,'group'=4] {'group'}, use_global_device_ids=true, to_apply=%region_16.17 | all-reduce | flops 2052 | bytes 16416 | tf_op jit(solution)/shard_map/psum | solution.py:89
  46.9 22.2 %all-reduce.9 = (f32[4,256]{1,0:T(4,128)S(1)}, f32[4]{0:T(128)S(1)}, f32[4,256]{1,0:T(4,128)S(1)}) all-reduce(f32[4,256]{1,0:T(4,128)S(1)} %get-tuple-element.34, f32[4]{0:T(128)S(1)} %get-tuple-element.35, f32[4,256]{1,0:T(4,128)S(1)} %get-tuple-element.36), channel_id=1, replica_groups=mesh['wide'=8,'group'=4] {'wide'}, use_global_device_ids=true, to_apply=%region_17.18 | all-reduce | flops 2052 | bytes 16416 | tf_op jit(solution)/shard_map/psum | solution.py:90
  69.7 2.4 slice_divide_fusion.8
  72.1 2.4 slice_divide_fusion.9
  77.6 0.7 fusion.299
  78.3 5.9 %all-reduce.10 = (f32[4,256]{1,0:T(4,128)S(1)}, f32[4,256]{1,0:T(4,128)S(1)}) all-reduce(f32[4,256]{1,0:T(4,128)S(1)} %pad_maximum_fusion.3, f32[4,256]{1,0:T(4,128)S(1)} %pad_maximum_fusion.2), channel_id=1, replica_groups=mesh['wide'=8,'group'=4] {'group'}, use_global_device_ids=true, to_apply=%region_28.29 | all-reduce | flops 2048 | bytes 16384 | tf_op jit(solution)/shard_map/psum | solution.py:89
  84.2 17.6 %all-reduce.8 = (f32[4,256]{1,0:T(4,128)S(1)}, f32[4,256]{1,0:T(4,128)S(1)}) all-reduce(f32[4,256]{1,0:T(4,128)S(1)} %get-tuple-element.32, f32[4,256]{1,0:T(4,128)S(1)} %get-tuple-element.33), channel_id=1, replica_groups=mesh['wide'=8,'group'=4] {'wide'}, use_global_device_ids=true, to_apply=%region_29.30 | all-reduce | flops 2048 | bytes 16384 | tf_op jit(solution)/shard_map/psum | solution.py:90
  101.8 2.4 slice_divide_fusion
  104.2 2.4 slice_divide_fusion.1
  106.7 1.1 multiply_convert_fusion.2
  119.8 2.1 add_add_fusion
  124.2 0.8 convolution_add_fusion.49
  126.1 49.5 %all-reduce.14.cloned.1.call-done = f32[3,3,256,256]{3,2,1,0:T(8,128)} async-done(((f32[3,3,256,256]{3,2,1,0:T(8,128)}), f32[3,3,256,256]{3,2,1,0:T(8,128)}) %all-reduce.14.cloned.1.call-update) | async-done | bytes 2359312 | tf_op jit(solution)/shard_map/psum | solution.py:95
  175.6 1.5 collective-permute-start
  177.0 0.7 pad_slice_fusion.16
  177.8 0.7 reshape.1163
  179.1 1.5 reshape.1132
  181.7 0.9 convolution_add_fusion.33
  182.6 0.8 convolution_add_fusion.32
  185.1 43.6 %collective-permute-done = f32[3,3,256,256]{3,2,1,0:T(8,128)} collective-permute-done((f32[3,3,256,256]{3,2,1,0:T(8,128)}, f32[3,3,256,256]{3,2,1,0:T(8,128)}, u32[]{:S(2)}, u32[]{:S(2)}) %collective-permute-start) | collective-permute-done | bytes 2359328 | tf_op jit(solution)/shard_map/ppermute | solution.py:13
  228.6 3.4 add.721
  232.0 1.5 collective-permute-start.1
  236.8 0.7 multiply_convert_fusion.21
  237.5 0.7 multiply_convert_fusion.13
  239.3 44.9 %collective-permute-done.1 = f32[3,3,256,256]{3,2,1,0:T(8,128)} collective-permute-done((f32[3,3,256,256]{3,2,1,0:T(8,128)}, f32[3,3,256,256]{3,2,1,0:T(8,128)}, u32[]{:S(2)}, u32[]{:S(2)}) %collective-permute-start.1) | collective-permute-done | bytes 2359328 | tf_op jit(solution)/shard_map/ppermute | solution.py:13
  284.2 2.7 add.722
  286.9 2.5 collective-permute-start.2
  289.4 0.8 multiply_convert_fusion.6
  292.5 1.1 multiply_convert_fusion.1
  293.6 95.9 %collective-permute-done.2 = f32[3,3,256,256]{3,2,1,0:T(8,128)S(1)} collective-permute-done((f32[3,3,256,256]{3,2,1,0:T(8,128)S(1)}, f32[3,3,256,256]{3,2,1,0:T(8,128)S(1)}, u32[]{:S(2)}, u32[]{:S(2)}) %collective-permute-start.2) | collective-permute-done | bytes 2359328 | tf_op jit(solution)/shard_map/ppermute | solution.py:13
  389.4 1.7 add_multiply_fusion
  (497 shorter events, 41.1 us)
Async XLA Ops:
  7.2 13.4 %copy-start = (bf16[3,3,256,256]{3,2,1,0:T(8,128)(2,1)S(1)}, bf16[3,3,256,256]{3,2,1,0:T(8,128)(2,1)}, u32[]{:S(2)}) copy-start(bf16[3,3,256,256]{3,2,1,0:T(8,128)(2,1)} %param.21) | copy-start | bytes 3538948
  7.2 16.6 %copy-start.7 = (bf16[1,12,12,256]{3,2,1,0:T(8,128)(2,1)S(1)}, bf16[1,12,12,256]{3,2,1,0:T(8,128)(2,1)}, u32[]{:S(2)}) copy-start(bf16[1,12,12,256]{3,2,1,0:T(8,128)(2,1)} %param.14) | copy-start | bytes 221188
  7.2 168.4 %all-reduce.14.cloned.1.call-start = ((), (), s32[]{:S(2)}) async-start(), calls=%async_computation | async-start | bytes 4718592 | tf_op jit(solution)/shard_map/psum | solution.py:95
  16.0 8.4 %copy-start.27 = (bf16[6,6,256]{2,1,0:T(8,128)(2,1)}, bf16[6,6,256]{2,1,0:T(8,128)(2,1)S(1)}, u32[]{:S(2)}) copy-start(bf16[6,6,256]{2,1,0:T(8,128)(2,1)S(1)} %bitcast_multiply_fusion.6) | copy-start | bytes 55300
  16.8 7.5 %copy-start.29 = (bf16[1,6,6,256]{3,2,1,0:T(8,128)(2,1)}, bf16[1,6,6,256]{3,2,1,0:T(8,128)(2,1)S(1)}, u32[]{:S(2)}) copy-start(bf16[1,6,6,256]{3,2,1,0:T(8,128)(2,1)S(1)} %broadcast_multiply_fusion.2) | copy-start | bytes 55300
  32.2 44.6 %copy-start.42 = (f32[1,256]{1,0:T(1,128)}, f32[1,256]{1,0:T(1,128)S(1)}, u32[]{:S(2)}) copy-start(f32[1,256]{1,0:T(1,128)S(1)} %get-tuple-element.118) | copy-start | bytes 3076
  32.2 45.0 %copy-start.61 = (f32[1,256]{1,0:T(1,128)}, f32[1,256]{1,0:T(1,128)S(1)}, u32[]{:S(2)}) copy-start(f32[1,256]{1,0:T(1,128)S(1)} %get-tuple-element.117) | copy-start | bytes 3076
  32.2 45.2 %copy-start.65 = (f32[1,256]{1,0:T(1,128)}, f32[1,256]{1,0:T(1,128)S(1)}, u32[]{:S(2)}) copy-start(f32[1,256]{1,0:T(1,128)S(1)} %get-tuple-element.119) | copy-start | bytes 3076
  32.2 45.3 %copy-start.98 = (f32[1,256]{1,0:T(1,128)}, f32[1,256]{1,0:T(1,128)S(1)}, u32[]{:S(2)}) copy-start(f32[1,256]{1,0:T(1,128)S(1)} %get-tuple-element.116) | copy-start | bytes 3076
  32.3 44.6 %copy-start.51 = (f32[1,256]{1,0:T(1,128)}, f32[1,256]{1,0:T(1,128)S(1)}, u32[]{:S(2)}) copy-start(f32[1,256]{1,0:T(1,128)S(1)} %get-tuple-element.130) | copy-start | bytes 3076
  32.3 45.0 %copy-start.83 = (f32[1,256]{1,0:T(1,128)}, f32[1,256]{1,0:T(1,128)S(1)}, u32[]{:S(2)}) copy-start(f32[1,256]{1,0:T(1,128)S(1)} %get-tuple-element.129) | copy-start | bytes 3076
  32.3 45.1 %copy-start.87 = (f32[1,256]{1,0:T(1,128)}, f32[1,256]{1,0:T(1,128)S(1)}, u32[]{:S(2)}) copy-start(f32[1,256]{1,0:T(1,128)S(1)} %get-tuple-element.131) | copy-start | bytes 3076
  32.3 45.3 %copy-start.101 = (f32[1,256]{1,0:T(1,128)}, f32[1,256]{1,0:T(1,128)S(1)}, u32[]{:S(2)}) copy-start(f32[1,256]{1,0:T(1,128)S(1)} %get-tuple-element.128) | copy-start | bytes 3076
  34.6 42.3 %copy-start.1 = (bf16[1,24,24,256]{3,2,1,0:T(8,128)(2,1)S(1)}, bf16[1,24,24,256]{3,2,1,0:T(8,128)(2,1)}, u32[]{:S(2)}) copy-start(bf16[1,24,24,256]{3,2,1,0:T(8,128)(2,1)} %param.17) | copy-start | bytes 884740
  34.6 42.3 %copy-start.16 = (f32[24,24]{1,0:T(8,128)S(1)}, f32[24,24]{1,0:T(8,128)}, u32[]{:S(2)}) copy-start(f32[24,24]{1,0:T(8,128)} %get-tuple-element.150) | copy-start | bytes 6916
  35.2 42.1 %copy-start.4 = (bf16[1,12,12,256]{3,2,1,0:T(8,128)(2,1)S(1)}, bf16[1,12,12,256]{3,2,1,0:T(8,128)(2,1)}, u32[]{:S(2)}) copy-start(bf16[1,12,12,256]{3,2,1,0:T(8,128)(2,1)} %param.18) | copy-start | bytes 221188
  35.2 42.3 %copy-start.14 = (bf16[1,6,6,256]{3,2,1,0:T(8,128)(2,1)S(1)}, bf16[1,6,6,256]{3,2,1,0:T(8,128)(2,1)}, u32[]{:S(2)}) copy-start(bf16[1,6,6,256]{3,2,1,0:T(8,128)(2,1)} %param.19) | copy-start | bytes 55300
  35.2 42.3 %copy-start.32 = (f32[6,6]{1,0:T(8,128)S(1)}, f32[6,6]{1,0:T(8,128)}, u32[]{:S(2)}) copy-start(f32[6,6]{1,0:T(8,128)} %get-tuple-element.146) | copy-start | bytes 436
  35.2 42.4 %copy-start.25 = (f32[3,3,256]{2,1,0:T(4,128)S(1)}, f32[3,3,256]{2,1,0:T(4,128)}, u32[]{:S(2)}) copy-start(f32[3,3,256]{2,1,0:T(4,128)} %reshape.1121) | copy-start | bytes 27652
  35.2 42.4 %copy-start.45 = (f32[3,3]{1,0:T(4,128)S(1)}, f32[3,3]{1,0:T(4,128)}, u32[]{:S(2)}) copy-start(f32[3,3]{1,0:T(4,128)} %get-tuple-element.144) | copy-start | bytes 112
  35.2 42.4 %copy-start.72 = (bf16[1,3,3,256]{3,2,1,0:T(4,128)(2,1)S(1)}, bf16[1,3,3,256]{3,2,1,0:T(4,128)(2,1)}, u32[]{:S(2)}) copy-start(bf16[1,3,3,256]{3,2,1,0:T(4,128)(2,1)} %param.20) | copy-start | bytes 13828
  74.5 32.1 %copy-start.39 = (f32[1,256]{1,0:T(1,128)}, f32[1,256]{1,0:T(1,128)S(1)}, u32[]{:S(2)}) copy-start(f32[1,256]{1,0:T(1,128)S(1)} %get-tuple-element.123) | copy-start | bytes 3076
  74.5 32.1 %copy-start.54 = (f32[1,256]{1,0:T(1,128)}, f32[1,256]{1,0:T(1,128)S(1)}, u32[]{:S(2)}) copy-start(f32[1,256]{1,0:T(1,128)S(1)} %get-tuple-element.122) | copy-start | bytes 3076
  74.5 32.1 %copy-start.58 = (f32[1,256]{1,0:T(1,128)}, f32[1,256]{1,0:T(1,128)S(1)}, u32[]{:S(2)}) copy-start(f32[1,256]{1,0:T(1,128)S(1)} %get-tuple-element.121) | copy-start | bytes 3076
  74.5 32.1 %copy-start.68 = (f32[1,256]{1,0:T(1,128)}, f32[1,256]{1,0:T(1,128)S(1)}, u32[]{:S(2)}) copy-start(f32[1,256]{1,0:T(1,128)S(1)} %get-tuple-element.120) | copy-start | bytes 3076
  75.1 31.5 %copy-start.80 = (f32[256]{0:T(256)}, f32[256]{0:T(256)S(1)}, u32[]{:S(2)}) copy-start(f32[256]{0:T(256)S(1)} %get-tuple-element.137) | copy-start | bytes 3076
  75.7 31.0 %copy-start.91 = (f32[256]{0:T(256)}, f32[256]{0:T(256)S(1)}, u32[]{:S(2)}) copy-start(f32[256]{0:T(256)S(1)} %get-tuple-element.135) | copy-start | bytes 3076
  76.3 30.4 %copy-start.76 = (f32[256]{0:T(256)}, f32[256]{0:T(256)S(1)}, u32[]{:S(2)}) copy-start(f32[256]{0:T(256)S(1)} %get-tuple-element.139) | copy-start | bytes 3076
  76.8 29.9 %copy-start.48 = (f32[256]{0:T(256)}, f32[256]{0:T(256)S(1)}, u32[]{:S(2)}) copy-start(f32[256]{0:T(256)S(1)} %get-tuple-element.141) | copy-start | bytes 3076
  104.2 5.0 %copy-start.106 = (f32[1,256]{1,0:T(1,128)}, f32[1,256]{1,0:T(1,128)S(1)}, u32[]{:S(2)}) copy-start(f32[1,256]{1,0:T(1,128)S(1)} %get-tuple-element.113) | copy-start | bytes 3076
  104.2 8.8 %copy-start.117 = (f32[1,256]{1,0:T(1,128)}, f32[1,256]{1,0:T(1,128)S(1)}, u32[]{:S(2)}) copy-start(f32[1,256]{1,0:T(1,128)S(1)} %get-tuple-element.111) | copy-start | bytes 3076
  104.2 11.4 %copy-start.126 = (f32[1,256]{1,0:T(1,128)}, f32[1,256]{1,0:T(1,128)S(1)}, u32[]{:S(2)}) copy-start(f32[1,256]{1,0:T(1,128)S(1)} %get-tuple-element.110) | copy-start | bytes 3076
  104.2 13.8 %copy-start.112 = (f32[1,256]{1,0:T(1,128)}, f32[1,256]{1,0:T(1,128)S(1)}, u32[]{:S(2)}) copy-start(f32[1,256]{1,0:T(1,128)S(1)} %get-tuple-element.112) | copy-start | bytes 3076
  106.6 6.4 %copy-start.119 = (f32[1,256]{1,0:T(1,128)}, f32[1,256]{1,0:T(1,128)S(1)}, u32[]{:S(2)}) copy-start(f32[1,256]{1,0:T(1,128)S(1)} %get-tuple-element.107) | copy-start | bytes 3076
  106.6 9.0 %copy-start.128 = (f32[1,256]{1,0:T(1,128)}, f32[1,256]{1,0:T(1,128)S(1)}, u32[]{:S(2)}) copy-start(f32[1,256]{1,0:T(1,128)S(1)} %get-tuple-element.106) | copy-start | bytes 3076
  106.6 11.4 %copy-start.114 = (f32[1,256]{1,0:T(1,128)}, f32[1,256]{1,0:T(1,128)S(1)}, u32[]{:S(2)}) copy-start(f32[1,256]{1,0:T(1,128)S(1)} %get-tuple-element.108) | copy-start | bytes 3076
  125.3 53.1 %copy-start.71 = (bf16[3,3,256]{2,1,0:T(4,128)(2,1)S(1)}, bf16[3,3,256]{2,1,0:T(4,128)(2,1)}, u32[]{:S(2)}) copy-start(bf16[3,3,256]{2,1,0:T(4,128)(2,1)} %get-tuple-element.90) | copy-start | bytes 13828
  175.6 53.1 %collective-permute-start = (f32[3,3,256,256]{3,2,1,0:T(8,128)}, f32[3,3,256,256]{3,2,1,0:T(8,128)}, u32[]{:S(2)}, u32[]{:S(2)}) collective-permute-start(f32[3,3,256,256]{3,2,1,0:T(8,128)} %all-reduce.14.cloned.1.call-done), channel_id=1, source_target_pairs={{0,4},{4,0},{8,12},{12,8},{16,20},{20,16},{24,28},{28,24},{1,5},{5... | collective-permute-start | bytes 7077896 | tf_op jit(solution)/shard_map/ppermute | solution.py:13
  184.1 44.6 %copy-start.2 = (f32[3,3,256,256]{3,2,1,0:T(8,128)S(1)}, f32[3,3,256,256]{3,2,1,0:T(8,128)}, u32[]{:S(2)}) copy-start(f32[3,3,256,256]{3,2,1,0:T(8,128)} %all-reduce.14.cloned.1.call-done) | copy-start | bytes 7077892
  185.0 48.5 %copy-start.31 = (f32[9,256]{1,0:T(8,128)S(1)}, f32[9,256]{1,0:T(8,128)}, u32[]{:S(2)}) copy-start(f32[9,256]{1,0:T(8,128)} %convolution_add_fusion.49) | copy-start | bytes 27652
  185.1 49.2 %copy-start.21 = (f32[36,256]{1,0:T(8,128)S(1)}, f32[36,256]{1,0:T(8,128)}, u32[]{:S(2)}) copy-start(f32[36,256]{1,0:T(8,128)} %convolution_add_fusion.32) | copy-start | bytes 110596
  232.0 52.2 %collective-permute-start.1 = (f32[3,3,256,256]{3,2,1,0:T(8,128)}, f32[3,3,256,256]{3,2,1,0:T(8,128)}, u32[]{:S(2)}, u32[]{:S(2)}) collective-permute-start(f32[3,3,256,256]{3,2,1,0:T(8,128)} %add.721), channel_id=1, source_target_pairs={{0,8},{4,12},{8,0},{12,4},{16,24},{20,28},{24,16},{28,20},{1,9},{5... | collective-permute-start | bytes 7077896 | tf_op jit(solution)/shard_map/ppermute | solution.py:13
  239.3 50.1 %copy-start.6 = (f32[1,12,12,256]{3,2,1,0:T(8,128)S(1)}, f32[1,12,12,256]{3,2,1,0:T(8,128)}, u32[]{:S(2)}) copy-start(f32[1,12,12,256]{3,2,1,0:T(8,128)} %reshape.1115) | copy-start | bytes 442372
  239.3 50.1 %copy-start.57 = (f32[1,256]{1,0:T(1,128)S(1)}, f32[1,256]{1,0:T(1,128)}, u32[]{:S(2)}) copy-start(f32[1,256]{1,0:T(1,128)} %copy-done.54) | copy-start | bytes 3076
  239.3 50.1 %copy-start.64 = (f32[1,256]{1,0:T(1,128)S(1)}, f32[1,256]{1,0:T(1,128)}, u32[]{:S(2)}) copy-start(f32[1,256]{1,0:T(1,128)} %copy-done.61) | copy-start | bytes 3076
  239.3 50.1 %copy-start.79 = (f32[256]{0:T(256)S(1)}, f32[256]{0:T(256)}, u32[]{:S(2)}) copy-start(f32[256]{0:T(256)} %copy-done.76) | copy-start | bytes 3076
  239.3 50.1 %copy-start.86 = (f32[1,256]{1,0:T(1,128)S(1)}, f32[1,256]{1,0:T(1,128)}, u32[]{:S(2)}) copy-start(f32[1,256]{1,0:T(1,128)} %copy-done.83) | copy-start | bytes 3076
  286.9 102.5 %collective-permute-start.2 = (f32[3,3,256,256]{3,2,1,0:T(8,128)S(1)}, f32[3,3,256,256]{3,2,1,0:T(8,128)S(1)}, u32[]{:S(2)}, u32[]{:S(2)}) collective-permute-start(f32[3,3,256,256]{3,2,1,0:T(8,128)S(1)} %add.722), channel_id=1, source_target_pairs={{0,16},{4,20},{8,24},{12,28},{16,0},{20,4},{24,8},{28,12},{1,17},{... | collective-permute-start | bytes 7077896 | tf_op jit(solution)/shard_map/ppermute | solution.py:13
  (91 other events, 187.9 us)
Sparse Core Ops, SparseCore 0:
  122.0 53.5 all-reduce.13
